TPU v7x, 512 devices: a 8x2x16 block of a 8x8x16 slice. The times are simulated.
512 devices in a mesh: groups: 2 (over y), section: 16 (over z), seq: 16 (over x, core).
Axes of the slice: x: 8, y: 2, z: 16, core: 2. Of those that a mesh axis runs over, the one named last changes fastest.
The devices are a block of a 8x8x16 slice.
Arguments:
- tokens: bfloat16 [8, 1024, 1440], P('groups', 'seq'), parts along dimension 0, may hold values from -6 to 6
- block_order: int32 [8], P('groups'), parts along dimension 0, may hold values from 0 to 3, each once
- prompt_lengths: int32 [8], P('groups'), parts along dimension 0, may hold values from 1 to 1024, 2304 in all
- norm_gain: float32 [16, 1440], P('section'), may hold values from 0.1 to 1.9
- w_query: bfloat16 [16, 1440, 2048], P('section', None, 'seq'), may hold values from -4 to 4
- w_key_value: bfloat16 [16, 1440, 512], P('section'), may hold values from -4 to 4
- w_out: bfloat16 [16, 2048, 1440], P('section', 'seq'), may hold values from -0.125 to 0.125
- sink_logits: float32 [16, 32], P('section'), may hold values from 0 to 4
Outputs:
- hidden_states: bfloat16 [16, 8, 1024, 1440], P('section', 'groups', 'seq'), parts along dimension 1
- layer_cache: bfloat16 [16, 8, 1024, 512], P('section', 'groups', 'seq'), parts along dimension 1
There are 2 independent parts, one for each index of `groups`. A program takes and returns all parts, laid end to end along the dimension named above; an argument that names none is the same for every part. Nothing has to cross between parts.
Inputs may be any that keep to these rules, and one draw needn't show every extreme that they name: `block_order`: each of 0 to 3 exactly once. `prompt_lengths`: the longest prompt is full.
All inputs are finite; a program needn't handle non-finite values.
Results may differ from a plain program's by a relative error of at most 0.024.
Values may be sent and summed in bfloat16 or wider, within the bound.
A program may use at most 128 MiB of HBM per device.

v0:
```python
import math
import jax
import jax.numpy as jnp
from jax import lax
from jax.sharding import PartitionSpec as P

HEAD_DIM = 64
WIN = 128
THETA = 150000.0
EPSILON = 1e-05


def rows_first(arrays, axis, dims):
    turned = [jnp.moveaxis(a, dim, 0) for a, dim in zip(arrays, dims)]
    widths = [t[0].size for t in turned]
    both = jnp.concatenate([t.reshape(-1, w) for t, w in zip(turned, widths)], axis=1)
    out = lax.all_gather(both, axis, axis=0, tiled=True)
    parts = jnp.split(out, [sum(widths[:k]) for k in range(1, len(widths))], axis=1)
    return tuple(
        (
            jnp.moveaxis(b.reshape(-1, *t.shape[1:]), 0, dim)
            for b, t, dim in zip(parts, turned, dims)
        )
    )


def from_behind(block, axis, distance):
    devices = range(lax.axis_size(axis))
    route = [(i - distance, i) for i in devices if i - distance in devices]
    return lax.ppermute(block, axis, route)


def rotary(positions, head_size):
    half = head_size // 2
    freq = jnp.exp(jnp.arange(half, dtype=jnp.float32) * (-2.0 * math.log(THETA) / head_size))
    angles = positions.astype(jnp.float32)[:, None] * freq[None, :]
    return (jnp.cos(angles)[:, None, :], jnp.sin(angles)[:, None, :])


def rotate(values, cosine, sine):
    half = values.shape[-1] // 2
    first = values[..., :half]
    second = values[..., half:]
    return jnp.concatenate([first * cosine - second * sine, second * cosine + first * sine], -1)


def per_device(
    tokens, block_order, prompt_lengths, norm_gain, w_query, w_key_value, w_out, sink_logits
):
    section_index = lax.axis_index("section")
    sections = lax.axis_size("section")
    seq_index = lax.axis_index("seq")
    micro, rows, width = tokens.shape
    full_query, full_out = rows_first((w_query, w_out), "seq", (2, 1))
    query_weight = full_query[0]
    out_weight = full_out[0]
    pair_weight = w_key_value[0]
    gain = norm_gain[0]
    heads_width = query_weight.shape[1]
    head_count = heads_width // HEAD_DIM
    kv_width = pair_weight.shape[1] // 2
    kv_heads = kv_width // HEAD_DIM
    group = head_count // kv_heads
    sink = sink_logits[0].reshape(kv_heads, group)[:, :, None]
    keep = min(WIN, rows)
    depth = WIN // keep
    start = seq_index * rows
    positions = start + jnp.arange(rows, dtype=jnp.int32)
    cosine, sine = rotary(positions, HEAD_DIM)
    key_positions = start - WIN + jnp.arange(WIN + rows, dtype=jnp.int32)

    def project(hidden):
        widened = hidden.astype(jnp.float32)
        scale = lax.rsqrt(jnp.mean(widened * widened, -1, keepdims=True) + EPSILON)
        normed = (widened * scale * gain).astype(jnp.bfloat16)
        queries = jnp.dot(normed, query_weight, preferred_element_type=jnp.float32).reshape(
            rows, head_count, HEAD_DIM
        )
        queries = rotate(queries, cosine, sine).astype(jnp.bfloat16).reshape(rows, heads_width)
        projected = jnp.dot(normed, pair_weight, preferred_element_type=jnp.float32)
        rotated = rotate(
            projected[:, :kv_width].reshape(rows, kv_heads, HEAD_DIM), cosine, sine
        ).reshape(rows, kv_width)
        cache = jnp.concatenate([rotated, projected[:, kv_width:]], 1).astype(jnp.bfloat16)
        return (queries, cache)

    def project_spare(hidden):
        return (
            jnp.zeros((rows, heads_width), jnp.bfloat16),
            jnp.zeros((rows, 2 * kv_width), jnp.bfloat16),
        )

    def window_of(cache):
        pieces = [from_behind(cache, "seq", offset) for offset in range(depth, 0, -1)]
        return jnp.concatenate(pieces, 0)

    def attend(operands):
        hidden, queries, cache, window, length = operands
        joined = jnp.concatenate([window, cache], 0)
        key_heads = joined[:, :kv_width].reshape(WIN + rows, kv_heads, HEAD_DIM)
        value_heads = joined[:, kv_width:].reshape(WIN + rows, kv_heads, HEAD_DIM)
        grouped = queries.reshape(rows, kv_heads, group, HEAD_DIM)
        scores = (
            jnp.einsum("qkgd,skd->kgqs", grouped, key_heads, preferred_element_type=jnp.float32)
            * 0.125
        )
        query_col = positions[:, None]
        key_row = key_positions[None, :]
        allowed = (key_row <= query_col) & (query_col - key_row < WIN) & (key_row >= 0)
        allowed = allowed & ((key_row < length) | (key_row == query_col))
        masked = jnp.where(allowed, scores, jnp.float32(-1e30))
        top = jnp.maximum(jnp.max(masked, -1), sink)
        expo = jnp.where(allowed, jnp.exp(scores - top[..., None]), jnp.float32(0.0))
        total = jnp.sum(expo, -1) + jnp.exp(sink - top)
        weights = (expo / total[..., None]).astype(jnp.bfloat16)
        context = jnp.einsum(
            "kgqs,skd->qkgd", weights, value_heads, preferred_element_type=jnp.float32
        )
        context = context.reshape(rows, heads_width).astype(jnp.bfloat16)
        output = jnp.dot(context, out_weight, preferred_element_type=jnp.float32)
        return (hidden.astype(jnp.float32) + output).astype(jnp.bfloat16)

    def pass_through(operands):
        return operands[0]

    def turn(counter, carry):
        arriving, hidden_buffer, cache_buffer = carry
        slot = counter - section_index
        active = (slot >= 0) & (slot < micro)
        slot_safe = jnp.clip(slot, 0, micro - 1)
        block = block_order[slot_safe]
        length = prompt_lengths[block]
        entering = lax.dynamic_index_in_dim(tokens, block, 0, keepdims=False)
        hidden = jnp.where(section_index == 0, entering, arriving)
        queries, cache = lax.cond(active, project, project_spare, hidden)
        window = window_of(cache)
        updated = lax.cond(active, attend, pass_through, (hidden, queries, cache, window, length))
        previous_hidden = lax.dynamic_index_in_dim(hidden_buffer, slot_safe, 0, keepdims=False)
        previous_cache = lax.dynamic_index_in_dim(cache_buffer, slot_safe, 0, keepdims=False)
        hidden_buffer = lax.dynamic_update_index_in_dim(
            hidden_buffer, jnp.where(active, updated, previous_hidden), slot_safe, 0
        )
        cache_buffer = lax.dynamic_update_index_in_dim(
            cache_buffer, jnp.where(active, cache, previous_cache), slot_safe, 0
        )
        passed = from_behind(updated, "section", 1)
        return (passed, hidden_buffer, cache_buffer)

    initial = (
        jnp.zeros((rows, width), jnp.bfloat16),
        jnp.zeros((micro, rows, width), jnp.bfloat16),
        jnp.zeros((micro, rows, 2 * kv_width), jnp.bfloat16),
    )
    final = lax.fori_loop(0, micro + sections - 1, turn, initial)
    return (final[1][None], final[2][None])


def solution(mesh):
    in_specs = (
        P("groups", "seq", None),
        P("groups"),
        P("groups"),
        P("section", None),
        P("section", None, "seq"),
        P("section", None, None),
        P("section", "seq", None),
        P("section", None),
    )
    out_specs = (P("section", "groups", "seq", None), P("section", "groups", "seq", None))
    return jax.shard_map(
        per_device, mesh=mesh, in_specs=in_specs, out_specs=out_specs, check_vma=False
    )
```

profile of v0, /device:TPU:1858, one launch (start us, length us, event | category | flops | bytes accessed | tf_op | source)
XLA Modules:
  0.0 783.1 jit_solution(16255271315744415141)
XLA Ops:
  10.6 83.0 %all-gather.2.cloned.1.call-done = bf16[2048,2880]{0,1:T(8,128)(2,1)} async-done(((bf16[128,2880]{0,1:T(8,128)(2,1)}), bf16[2048,2880]{0,1:T(8,128)(2,1)}) %all-gather.2.cloned.1.call-update) | async-done | bytes 11796496 | tf_op jit(solution)/shard_map/all_gather | solution.py:17
  93.6 10.2 %fusion.29 = (bf16[2048,1440]{0,1:T(8,128)(2,1)}, bf16[1440,2048]{1,0:T(8,128)(2,1)}) fusion(bf16[2048,2880]{0,1:T(8,128)(2,1)} %all-gather.2.cloned.1.call-done), kind=kLoop, calls=%fused_computation.61 | loop fusion | bytes 23592960 | tf_op jit(solution)/shard_map/split | solution.py:18
  103.8 8.7 %copy.20 = bf16[2048,1440]{1,0:T(8,128)(2,1)} copy(bf16[2048,1440]{0,1:T(8,128)(2,1)} %get-tuple-element.613) | data formatting | bytes 11796480
  114.2 662.0 %while.20 = (s32[]{:T(128)}, bf16[64,1440]{1,0:T(8,128)(2,1)S(1)}, bf16[4,64,1440]{2,1,0:T(8,128)(2,1)}, bf16[4,64,512]{2,1,0:T(8,128)(2,1)}, s32[]{:T(128)}, /*...) while((s32[]{:T(128)}, bf16[64,1440]{1,0:T(8,128)(2,1)S(1)}, ...), condition=%wide.region_8.9_spmd.clone.clone, body=%wide.region_0.8_spmd.clone.clone.sunk | while | flops 958372544 | bytes 48405112 | solution.py:154
  131.1 4.2 collective-permute-done.2
  152.7 4.2 collective-permute-done.2
  160.9 4.0 collective-permute-start
  174.8 4.3 collective-permute-done.2
  196.7 5.5 collective-permute-done.2
  218.5 6.1 collective-permute-done.2
  241.0 6.1 collective-permute-done.2
  263.5 6.1 collective-permute-done.2
  286.1 6.1 collective-permute-done.2
  308.6 6.1 collective-permute-done.2
  331.1 6.1 collective-permute-done.2
  353.6 6.1 collective-permute-done.2
  376.1 6.1 collective-permute-done.2
  398.6 6.1 collective-permute-done.2
  421.1 176.7 %collective-permute-done.2 = bf16[64,1440]{1,0:T(8,128)(2,1)S(1)} collective-permute-done((bf16[64,1440]{1,0:T(8,128)(2,1)S(1)}, bf16[64,1440]{1,0:T(8,128)(2,1)S(1)}, u32[]{:S(2)}, u32[]{:S(2)}) %collective-permute-start.2) | collective-permute-done | bytes 184352 | tf_op jit(solution)/shard_map/while/body/eval_jaxpr/ppermute | solution.py:30
  601.1 7.7 conditional.8
  618.6 7.1 conditional.9
  628.4 6.1 collective-permute-done.2
  637.8 7.7 conditional.8
  655.2 7.1 conditional.9
  665.0 6.1 collective-permute-done.2
  674.5 7.7 conditional.8
  691.9 7.1 conditional.9
  701.7 6.1 collective-permute-done.2
  711.1 7.7 conditional.8
  728.6 7.1 conditional.9
  738.3 4.9 collective-permute-done.2
  756.7 16.4 %collective-permute-start.2 = (bf16[64,1440]{1,0:T(8,128)(2,1)S(1)}, bf16[64,1440]{1,0:T(8,128)(2,1)S(1)}, u32[]{:S(2)}, u32[]{:S(2)}) collective-permute-start(bf16[64,1440]{1,0:T(8,128)(2,1)S(1)} %get-tuple-element.802), channel_id=1, source_target_pairs={{0,16},{16,32},{32,48},{48,64},{64,80},{80,96},{96,112},{112,128},... | collective-permute-start | bytes 552968 | tf_op jit(solution)/shard_map/while/body/eval_jaxpr/ppermute | solution.py:30
  (529 shorter events, 350.1 us)
Async XLA Ops:
  7.2 86.4 %all-gather.2.cloned.1.call-start = ((), (), s32[]{:S(2)}) async-start(), calls=%async_computation | async-start | bytes 12533760 | tf_op jit(solution)/shard_map/all_gather | solution.py:17
  118.3 7.8 collective-permute-start
  139.3 7.8 collective-permute-start
  160.9 8.4 %collective-permute-start = (bf16[64,512]{0,1:T(8,128)(2,1)}, bf16[64,512]{0,1:T(8,128)(2,1)S(1)}, u32[]{:S(2)}, u32[]{:S(2)}) collective-permute-start(bf16[64,512]{0,1:T(8,128)(2,1)} %get-tuple-element.727), channel_id=1, source_target_pairs={{0,2},{1,3},{2,4},{3,5},{4,6},{5,7},{6,8},{7,9},{8,10},{9,11},{10,... | collective-permute-start | bytes 196616 | tf_op jit(solution)/shard_map/while/body/eval_jaxpr/ppermute | solution.py:30
  171.4 7.7 collective-permute-start.2
  183.1 8.1 %collective-permute-start = (bf16[64,512]{0,1:T(8,128)(2,1)}, bf16[64,512]{0,1:T(8,128)(2,1)S(1)}, u32[]{:S(2)}, u32[]{:S(2)}) collective-permute-start(bf16[64,512]{0,1:T(8,128)(2,1)} %get-tuple-element.727), channel_id=1, source_target_pairs={{0,2},{1,3},{2,4},{3,5},{4,6},{5,7},{6,8},{7,9},{8,10},{9,11},{10,... | collective-permute-start | bytes 196616 | tf_op jit(solution)/shard_map/while/body/eval_jaxpr/ppermute | solution.py:30
  193.3 8.8 %collective-permute-start.2 = (bf16[64,1440]{1,0:T(8,128)(2,1)S(1)}, bf16[64,1440]{1,0:T(8,128)(2,1)S(1)}, u32[]{:S(2)}, u32[]{:S(2)}) collective-permute-start(bf16[64,1440]{1,0:T(8,128)(2,1)S(1)} %get-tuple-element.802), channel_id=1, source_target_pairs={{0,16},{16,32},{32,48},{48,64},{64,80},{80,96},{96,112},{112,128},... | collective-permute-start | bytes 552968 | tf_op jit(solution)/shard_map/while/body/eval_jaxpr/ppermute | solution.py:30
  206.1 7.6 collective-permute-start
  215.8 8.8 %collective-permute-start.2 = (bf16[64,1440]{1,0:T(8,128)(2,1)S(1)}, bf16[64,1440]{1,0:T(8,128)(2,1)S(1)}, u32[]{:S(2)}, u32[]{:S(2)}) collective-permute-start(bf16[64,1440]{1,0:T(8,128)(2,1)S(1)} %get-tuple-element.802), channel_id=1, source_target_pairs={{0,16},{16,32},{32,48},{48,64},{64,80},{80,96},{96,112},{112,128},... | collective-permute-start | bytes 552968 | tf_op jit(solution)/shard_map/while/body/eval_jaxpr/ppermute | solution.py:30
  228.6 7.6 collective-permute-start
  238.4 8.8 %collective-permute-start.2 = (bf16[64,1440]{1,0:T(8,128)(2,1)S(1)}, bf16[64,1440]{1,0:T(8,128)(2,1)S(1)}, u32[]{:S(2)}, u32[]{:S(2)}) collective-permute-start(bf16[64,1440]{1,0:T(8,128)(2,1)S(1)} %get-tuple-element.802), channel_id=1, source_target_pairs={{0,16},{16,32},{32,48},{48,64},{64,80},{80,96},{96,112},{112,128},... | collective-permute-start | bytes 552968 | tf_op jit(solution)/shard_map/while/body/eval_jaxpr/ppermute | solution.py:30
  251.2 7.6 collective-permute-start
  260.9 8.8 %collective-permute-start.2 = (bf16[64,1440]{1,0:T(8,128)(2,1)S(1)}, bf16[64,1440]{1,0:T(8,128)(2,1)S(1)}, u32[]{:S(2)}, u32[]{:S(2)}) collective-permute-start(bf16[64,1440]{1,0:T(8,128)(2,1)S(1)} %get-tuple-element.802), channel_id=1, source_target_pairs={{0,16},{16,32},{32,48},{48,64},{64,80},{80,96},{96,112},{112,128},... | collective-permute-start | bytes 552968 | tf_op jit(solution)/shard_map/while/body/eval_jaxpr/ppermute | solution.py:30
  273.7 7.6 collective-permute-start
  283.4 8.8 %collective-permute-start.2 = (bf16[64,1440]{1,0:T(8,128)(2,1)S(1)}, bf16[64,1440]{1,0:T(8,128)(2,1)S(1)}, u32[]{:S(2)}, u32[]{:S(2)}) collective-permute-start(bf16[64,1440]{1,0:T(8,128)(2,1)S(1)} %get-tuple-element.802), channel_id=1, source_target_pairs={{0,16},{16,32},{32,48},{48,64},{64,80},{80,96},{96,112},{112,128},... | collective-permute-start | bytes 552968 | tf_op jit(solution)/shard_map/while/body/eval_jaxpr/ppermute | solution.py:30
  296.2 7.6 collective-permute-start
  305.9 8.8 %collective-permute-start.2 = (bf16[64,1440]{1,0:T(8,128)(2,1)S(1)}, bf16[64,1440]{1,0:T(8,128)(2,1)S(1)}, u32[]{:S(2)}, u32[]{:S(2)}) collective-permute-start(bf16[64,1440]{1,0:T(8,128)(2,1)S(1)} %get-tuple-element.802), channel_id=1, source_target_pairs={{0,16},{16,32},{32,48},{48,64},{64,80},{80,96},{96,112},{112,128},... | collective-permute-start | bytes 552968 | tf_op jit(solution)/shard_map/while/body/eval_jaxpr/ppermute | solution.py:30
  328.4 8.8 %collective-permute-start.2 = (bf16[64,1440]{1,0:T(8,128)(2,1)S(1)}, bf16[64,1440]{1,0:T(8,128)(2,1)S(1)}, u32[]{:S(2)}, u32[]{:S(2)}) collective-permute-start(bf16[64,1440]{1,0:T(8,128)(2,1)S(1)} %get-tuple-element.802), channel_id=1, source_target_pairs={{0,16},{16,32},{32,48},{48,64},{64,80},{80,96},{96,112},{112,128},... | collective-permute-start | bytes 552968 | tf_op jit(solution)/shard_map/while/body/eval_jaxpr/ppermute | solution.py:30
  350.9 8.8 %collective-permute-start.2 = (bf16[64,1440]{1,0:T(8,128)(2,1)S(1)}, bf16[64,1440]{1,0:T(8,128)(2,1)S(1)}, u32[]{:S(2)}, u32[]{:S(2)}) collective-permute-start(bf16[64,1440]{1,0:T(8,128)(2,1)S(1)} %get-tuple-element.802), channel_id=1, source_target_pairs={{0,16},{16,32},{32,48},{48,64},{64,80},{80,96},{96,112},{112,128},... | collective-permute-start | bytes 552968 | tf_op jit(solution)/shard_map/while/body/eval_jaxpr/ppermute | solution.py:30
  363.7 7.6 collective-permute-start
  373.4 8.8 %collective-permute-start.2 = (bf16[64,1440]{1,0:T(8,128)(2,1)S(1)}, bf16[64,1440]{1,0:T(8,128)(2,1)S(1)}, u32[]{:S(2)}, u32[]{:S(2)}) collective-permute-start(bf16[64,1440]{1,0:T(8,128)(2,1)S(1)} %get-tuple-element.802), channel_id=1, source_target_pairs={{0,16},{16,32},{32,48},{48,64},{64,80},{80,96},{96,112},{112,128},... | collective-permute-start | bytes 552968 | tf_op jit(solution)/shard_map/while/body/eval_jaxpr/ppermute | solution.py:30
  395.9 8.8 %collective-permute-start.2 = (bf16[64,1440]{1,0:T(8,128)(2,1)S(1)}, bf16[64,1440]{1,0:T(8,128)(2,1)S(1)}, u32[]{:S(2)}, u32[]{:S(2)}) collective-permute-start(bf16[64,1440]{1,0:T(8,128)(2,1)S(1)} %get-tuple-element.802), channel_id=1, source_target_pairs={{0,16},{16,32},{32,48},{48,64},{64,80},{80,96},{96,112},{112,128},... | collective-permute-start | bytes 552968 | tf_op jit(solution)/shard_map/while/body/eval_jaxpr/ppermute | solution.py:30
  418.5 179.4 %collective-permute-start.2 = (bf16[64,1440]{1,0:T(8,128)(2,1)S(1)}, bf16[64,1440]{1,0:T(8,128)(2,1)S(1)}, u32[]{:S(2)}, u32[]{:S(2)}) collective-permute-start(bf16[64,1440]{1,0:T(8,128)(2,1)S(1)} %get-tuple-element.802), channel_id=1, source_target_pairs={{0,16},{16,32},{32,48},{48,64},{64,80},{80,96},{96,112},{112,128},... | collective-permute-start | bytes 552968 | tf_op jit(solution)/shard_map/while/body/eval_jaxpr/ppermute | solution.py:30
  608.9 7.6 collective-permute-start
  625.7 8.8 %collective-permute-start.2 = (bf16[64,1440]{1,0:T(8,128)(2,1)S(1)}, bf16[64,1440]{1,0:T(8,128)(2,1)S(1)}, u32[]{:S(2)}, u32[]{:S(2)}) collective-permute-start(bf16[64,1440]{1,0:T(8,128)(2,1)S(1)} %get-tuple-element.802), channel_id=1, source_target_pairs={{0,16},{16,32},{32,48},{48,64},{64,80},{80,96},{96,112},{112,128},... | collective-permute-start | bytes 552968 | tf_op jit(solution)/shard_map/while/body/eval_jaxpr/ppermute | solution.py:30
  645.5 7.6 collective-permute-start
  662.4 8.8 %collective-permute-start.2 = (bf16[64,1440]{1,0:T(8,128)(2,1)S(1)}, bf16[64,1440]{1,0:T(8,128)(2,1)S(1)}, u32[]{:S(2)}, u32[]{:S(2)}) collective-permute-start(bf16[64,1440]{1,0:T(8,128)(2,1)S(1)} %get-tuple-element.802), channel_id=1, source_target_pairs={{0,16},{16,32},{32,48},{48,64},{64,80},{80,96},{96,112},{112,128},... | collective-permute-start | bytes 552968 | tf_op jit(solution)/shard_map/while/body/eval_jaxpr/ppermute | solution.py:30
  682.2 7.6 collective-permute-start
  699.0 8.8 %collective-permute-start.2 = (bf16[64,1440]{1,0:T(8,128)(2,1)S(1)}, bf16[64,1440]{1,0:T(8,128)(2,1)S(1)}, u32[]{:S(2)}, u32[]{:S(2)}) collective-permute-start(bf16[64,1440]{1,0:T(8,128)(2,1)S(1)} %get-tuple-element.802), channel_id=1, source_target_pairs={{0,16},{16,32},{32,48},{48,64},{64,80},{80,96},{96,112},{112,128},... | collective-permute-start | bytes 552968 | tf_op jit(solution)/shard_map/while/body/eval_jaxpr/ppermute | solution.py:30
  718.8 7.6 collective-permute-start
  735.7 7.6 collective-permute-start.2
  756.7 19.5 %collective-permute-start.2 = (bf16[64,1440]{1,0:T(8,128)(2,1)S(1)}, bf16[64,1440]{1,0:T(8,128)(2,1)S(1)}, u32[]{:S(2)}, u32[]{:S(2)}) collective-permute-start(bf16[64,1440]{1,0:T(8,128)(2,1)S(1)} %get-tuple-element.802), channel_id=1, source_target_pairs={{0,16},{16,32},{32,48},{48,64},{64,80},{80,96},{96,112},{112,128},... | collective-permute-start | bytes 552968 | tf_op jit(solution)/shard_map/while/body/eval_jaxpr/ppermute | solution.py:30
  (47 other events, 262.2 us)
Sparse Core Ops, SparseCore 0:
  10.7 82.9 all-gather.1
where the time goes:
time: 788 us; the launch traced here: 783 us
  waiting for transfers between devices  399 us (51%)
  starting transfers between devices  153 us (19%)
  local copies, waits for them, and re-layouts  94.3 us (12%)
  other arithmetic  60.3 us (8%)
  loops' own time  34.1 us (4%)
  matrix products  28.7 us (4%)
  between operations  14.1 us (2%)
    ppermute x57, waiting for transfers between devices, from_behind(): return lax.ppermute(block, axis, route)  316 us
    ppermute x57, starting transfers between devices, from_behind(): return lax.ppermute(block, axis, route)  152 us
    all_gather x1, waiting for transfers between devices, rows_first(): out = lax.all_gather(both, axis, axis=0, tiled=True)  83 us
    another operation x1, loops' own time, per_device(): final = lax.fori_loop(0, micro + sections - 1, turn, initial)  32.9 us
    select_n x19, other arithmetic, turn(): hidden = jnp.where(section_index == 0, entering, arriving)  18.1 us
    dynamic_slice x19, local copies, waits for them, and re-layouts, turn(): lax.dynamic_index_in_dim(hidden_buffer, slot_safe, 0, keepdims=False)  18 us
    dynamic_slice x19, local copies, waits for them, and re-layouts, turn(): lax.dynamic_index_in_dim(cache_buffer, slot_safe, 0, keepdims=False)  16.2 us
  transfers between devices with their start and end apart: 58, of which 40 were waited for; matrix products, arithmetic and copies ran while one was open for 8% of the time, Pallas kernels for 0%

commit v1 on v0

--- a/solution.py
+++ b/solution.py
@@ -8,13 +8,16 @@
 WIN = 128
 THETA = 150000.0
 EPSILON = 1e-05
+lay_signs = lambda load, bus_axis, dimension_no: jnp.concatenate(
+    lax.all_to_all(jnp.stack(lax.psum(1, bus_axis) * [load]), bus_axis, 0, 0), axis=dimension_no
+)
 
 
 def rows_first(arrays, axis, dims):
     turned = [jnp.moveaxis(a, dim, 0) for a, dim in zip(arrays, dims)]
     widths = [t[0].size for t in turned]
     both = jnp.concatenate([t.reshape(-1, w) for t, w in zip(turned, widths)], axis=1)
-    out = lax.all_gather(both, axis, axis=0, tiled=True)
+    out = lay_signs(both, axis, 0)
     parts = jnp.split(out, [sum(widths[:k]) for k in range(1, len(widths))], axis=1)
     return tuple(
         (

time: 788 us -> 997 us (1.27)
  the two profiles are of different devices: /device:TPU:1858 before, /device:TPU:1857 now
where the time goes in v1:
time: 997 us; the launch traced here: 992 us
  waiting for transfers between devices  540 us (54%)
  starting transfers between devices  214 us (21%)
  local copies, waits for them, and re-layouts  110 us (11%)
  other arithmetic  59.8 us (6%)
  loops' own time  38.5 us (4%)
  matrix products  28.8 us (3%)
    ppermute x57, waiting for transfers between devices, from_behind(): return lax.ppermute(block, axis, route)  285 us
    all_to_all x1, waiting for transfers between devices, lax.all_to_all(jnp.stack(lax.psum(1, bus_axis) * [load]), bus_axis, 0, 0)  255 us
    ppermute x57, starting transfers between devices, from_behind(): return lax.ppermute(block, axis, route)  206 us
    another operation x1, loops' own time, per_device(): final = lax.fori_loop(0, micro + sections - 1, turn, initial)  37.1 us
  transfers between devices with their start and end apart: 58, of which 20 were waited for; matrix products, arithmetic and copies ran while one was open for 6% of the time, Pallas kernels for 0%

profile of v1, /device:TPU:1857, one launch (start us, length us, event | category | flops | bytes accessed | tf_op | source)
XLA Modules:
  0.0 992.1 jit_solution(12271100328495539944)
XLA Ops:
  1.8 6.6 stack.2
  8.4 8.1 all-to-all-start
  17.7 255.1 %all-to-all-done = bf16[16,128,2880]{1,2,0:T(8,128)(2,1)} async-done(((bf16[16,128,2880]{1,2,0:T(8,128)(2,1)}), bf16[16,128,2880]{1,2,0:T(8,128)(2,1)}, u32[]{:S(2)}, u32[]{:S(2)}) %all-to-all-start) | async-done | bytes 11796512 | tf_op jit(solution)/shard_map/all_to_all | solution.py:12
  272.8 6.3 copy_bitcast_fusion
  283.7 8.7 copy.25
  294.1 698.0 %while.20 = (s32[]{:T(128)}, bf16[64,1440]{1,0:T(8,128)(2,1)S(1)}, bf16[4,64,1440]{2,1,0:T(8,128)(2,1)}, bf16[4,64,512]{2,1,0:T(8,128)(2,1)}, s32[]{:T(128)}, /*...) while((s32[]{:T(128)}, bf16[64,1440]{1,0:T(8,128)(2,1)S(1)}, ...), condition=%wide.region_8.9_spmd.clone.clone, body=%wide.region_0.8_spmd.clone.clone.sunk | while | flops 958372544 | bytes 48406292 | solution.py:157
  474.4 5.8 collective-permute-start.1
  497.0 5.8 collective-permute-start.1
  519.6 5.8 collective-permute-start.1
  530.6 6.1 collective-permute-done.2
  542.3 5.8 collective-permute-start.1
  553.2 6.1 collective-permute-done.2
  564.9 5.8 collective-permute-start.1
  575.9 6.1 collective-permute-done.2
  587.5 5.8 collective-permute-start.1
  598.5 205.8 %collective-permute-done.2 = bf16[64,1440]{1,0:T(8,128)(2,1)S(1)} collective-permute-done((bf16[64,1440]{1,0:T(8,128)(2,1)S(1)}, bf16[64,1440]{1,0:T(8,128)(2,1)S(1)}, u32[]{:S(2)}, u32[]{:S(2)}) %collective-permute-start.2) | collective-permute-done | bytes 184352 | tf_op jit(solution)/shard_map/while/body/eval_jaxpr/ppermute | solution.py:33
  807.8 7.8 conditional.8
  817.0 5.7 collective-permute-start.1
  825.2 8.8 conditional.9
  836.7 6.1 collective-permute-done.2
  846.3 7.8 conditional.8
  855.4 5.7 collective-permute-start.1
  863.7 8.8 conditional.9
  875.2 6.1 collective-permute-done.2
  884.8 7.8 conditional.8
  893.9 5.7 collective-permute-start.1
  902.2 8.8 conditional.9
  913.7 6.1 collective-permute-done.2
  923.2 7.8 conditional.8
  932.4 5.7 collective-permute-start.1
  940.6 8.8 conditional.9
  970.6 17.8 %collective-permute-start.2 = (bf16[64,1440]{1,0:T(8,128)(2,1)S(1)}, bf16[64,1440]{1,0:T(8,128)(2,1)S(1)}, u32[]{:S(2)}, u32[]{:S(2)}) collective-permute-start(bf16[64,1440]{1,0:T(8,128)(2,1)S(1)} %get-tuple-element.831), channel_id=1, source_target_pairs={{0,16},{16,32},{32,48},{48,64},{64,80},{80,96},{96,112},{112,128},... | collective-permute-start | bytes 552968 | tf_op jit(solution)/shard_map/while/body/eval_jaxpr/ppermute | solution.py:33
  (642 shorter events, 362.5 us)
Async XLA Ops:
  8.4 264.4 %all-to-all-start = ((bf16[16,128,2880]{1,2,0:T(8,128)(2,1)}), bf16[16,128,2880]{1,2,0:T(8,128)(2,1)}, u32[]{:S(2)}, u32[]{:S(2)}) async-start(bf16[16,128,2880]{1,2,0:T(8,128)(2,1)} %stack.2), calls=%async_computation | async-start | bytes 23592960 | tf_op jit(solution)/shard_map/all_to_all | solution.py:12
  298.4 8.4 collective-permute-start
  306.9 9.1 collective-permute-start.2
  320.2 10.3 %collective-permute-start = (bf16[64,512]{0,1:T(8,128)(2,1)S(1)}, bf16[64,512]{0,1:T(8,128)(2,1)S(1)}, u32[]{:S(2)}, u32[]{:S(2)}) collective-permute-start(bf16[64,512]{0,1:T(8,128)(2,1)S(1)} %get-tuple-element.756), channel_id=1, source_target_pairs={{0,2},{1,3},{2,4},{3,5},{4,6},{5,7},{6,8},{7,9},{8,10},{9,11},{10,... | collective-permute-start | bytes 196616 | tf_op jit(solution)/shard_map/while/body/eval_jaxpr/ppermute | solution.py:33
  330.5 8.8 collective-permute-start.2
  343.7 9.9 collective-permute-start
  365.1 9.8 collective-permute-start
  387.2 9.2 collective-permute-start
  408.6 9.2 collective-permute-start
  430.0 9.2 collective-permute-start
  451.4 9.2 collective-permute-start
  473.0 9.5 collective-permute-start
  482.6 8.8 collective-permute-start.2
  495.7 9.5 collective-permute-start
  505.3 8.8 collective-permute-start.2
  518.3 9.5 collective-permute-start
  527.9 8.8 collective-permute-start.2
  540.9 9.5 collective-permute-start
  550.5 8.8 collective-permute-start.2
  563.6 9.5 collective-permute-start
  573.2 8.8 collective-permute-start.2
  586.2 9.5 collective-permute-start
  595.8 208.5 %collective-permute-start.2 = (bf16[64,1440]{1,0:T(8,128)(2,1)S(1)}, bf16[64,1440]{1,0:T(8,128)(2,1)S(1)}, u32[]{:S(2)}, u32[]{:S(2)}) collective-permute-start(bf16[64,1440]{1,0:T(8,128)(2,1)S(1)} %get-tuple-element.831), channel_id=1, source_target_pairs={{0,16},{16,32},{32,48},{48,64},{64,80},{80,96},{96,112},{112,128},... | collective-permute-start | bytes 552968 | tf_op jit(solution)/shard_map/while/body/eval_jaxpr/ppermute | solution.py:33
  815.7 9.5 collective-permute-start
  834.1 8.7 collective-permute-start.2
  854.1 9.5 collective-permute-start
  872.5 8.7 collective-permute-start.2
  892.6 9.5 collective-permute-start
  911.0 8.7 collective-permute-start.2
  931.1 9.5 collective-permute-start
  961.3 9.2 collective-permute-start
  970.6 21.5 %collective-permute-start.2 = (bf16[64,1440]{1,0:T(8,128)(2,1)S(1)}, bf16[64,1440]{1,0:T(8,128)(2,1)S(1)}, u32[]{:S(2)}, u32[]{:S(2)}) collective-permute-start(bf16[64,1440]{1,0:T(8,128)(2,1)S(1)} %get-tuple-element.831), channel_id=1, source_target_pairs={{0,16},{16,32},{32,48},{48,64},{64,80},{80,96},{96,112},{112,128},... | collective-permute-start | bytes 552968 | tf_op jit(solution)/shard_map/while/body/eval_jaxpr/ppermute | solution.py:33
  (103 other events, 1166.4 us)
